TPU v7x, 128 devices: a whole 4x4x4 slice. The times are simulated.
128 devices in a mesh: comp: 2 (over x_lo), tile: 64 (over y, z, x_hi, core).
Axes of the slice: x: 4 (x_hi: 2, x_lo: 2; x = x_hi * 2 + x_lo), y: 4, z: 4, core: 2. Of those that a mesh axis runs over, the one named last changes fastest.
Arguments:
- starting_perturbation: float32 [2, 128, 512, 512], P('comp', None, 'tile'), may hold values from -6 to 6
- measured_discrepancy: float32 [2, 128, 512, 512], P('comp', None, 'tile'), may hold values from -6 to 6
- diffusion: float32 [2, 128, 512, 512], P('comp', None, 'tile'), may hold values from 0.02 to 0.24
- vert_mix: float32 [2, 128, 128], P('comp'), may hold values from -0.03125 to 0.03125
- ocean_mask: int32 [512, 512], P('tile'), may hold values 0 or 1
- pair_tile: int32 [2, 64, 8], replicated, may hold values from 0 to 63, as said below
- pair_patch: int32 [2, 64, 64], replicated, may hold values from 0 to 31
- dest_patch: int32 [2, 64, 64], P('comp', 'tile'), may hold values from 0 to 31
- pair_blocks: int32 [2, 64, 8], P('comp', 'tile'), may hold values from 1 to 8, 48 in all within a row
- remap_weight: float32 [2, 4096, 128, 128], P('comp', 'tile'), may hold values from -0.5 to 0.5
Outputs:
- final_perturbation: float32 [2, 128, 512, 512], P('comp', None, 'tile')
- gradient: float32 [2, 128, 512, 512], P('comp', None, 'tile')
Inputs may be any that keep to these rules, and one draw needn't show every extreme that they name: `pair_tile`: the 8 source tiles listed for destination tile t are distinct; exactly one of them is (t + 32) mod 64, and each other is (t + o) mod 64 for some o from 1 - 8 to 7. A pair's live blocks are its first pair_blocks ones.
All inputs are finite; a program needn't handle non-finite values. No bound on the sum of `ocean_mask` on one device may be relied on, other than what follows from the above.
Results may differ from a plain program's by a relative error of at most 0.0001.
Values sent between devices are 32-bit elements; how exact they have to be, the bound alone decides.
A program may use at most 128 MiB of HBM per device.

v0:
```python
import jax
import jax.numpy as jnp
from jax import lax
from jax.experimental import pallas as pl
from jax.experimental.pallas import tpu as pltpu
from jax.sharding import PartitionSpec as P

STEPS = 4
LANES = 128
NEAR = 8
FAR = 2 * NEAR - 1

F32 = jnp.float32
BF16 = jnp.bfloat16


def halves(x):
    high = x.astype(BF16)
    return high, (x - high.astype(F32)).astype(BF16)


def mm(a, b):
    return jnp.dot(a, b, preferred_element_type=F32)


def window_kernel(
    tiles,
    start_hbm,
    measured_hbm,
    scaled_hbm,
    weight_hbm,
    sea_ref,
    mix_ref,
    source_col,
    source_row,
    landing_col,
    final_hbm,
    adjoint_hbm,
    v,
    w,
    g,
    scaled,
    measured,
    weights,
    mixed,
    forward_mix,
    forward_low,
    backward_mix,
    backward_low,
    outgoing,
    halo,
    surface,
    arrived,
    parcels,
    returned,
    picked,
    terms,
    load_sem,
    store_sem,
    halo_send,
    halo_recv,
    out_send,
    out_recv,
    back_send,
    back_recv,
):
    rows, levels, lon = scaled.shape
    chunks = lon // LANES
    patches = rows * chunks
    blocks = weights.shape[0]
    slots = 2 * NEAR
    last = rows - 1
    me = lax.axis_index("tile")
    other = 1 - lax.axis_index("comp")
    above = lax.rem(me + tiles - 1, tiles)
    below = lax.rem(me + 1, tiles)
    offsets = [j if j < NEAR else (tiles // 2 if j == FAR else j - FAR) for j in range(slots)]
    keep = (
        jnp.where(me > 0, 1.0, 0.0).astype(F32),
        jnp.where(me < tiles - 1, 1.0, 0.0).astype(F32),
    )

    loads = [
        pltpu.make_async_copy(start_hbm, v.at[0], load_sem.at[0]),
        pltpu.make_async_copy(scaled_hbm, scaled, load_sem.at[1]),
        pltpu.make_async_copy(weight_hbm, weights, load_sem.at[2]),
        pltpu.make_async_copy(measured_hbm, measured, load_sem.at[3]),
    ]
    for load in loads:
        load.start()

    barrier = pltpu.get_barrier_semaphore()
    for neighbour in (above, below):
        pl.semaphore_signal(barrier, inc=1, device_id={"tile": neighbour})
    for offset in offsets:
        pl.semaphore_signal(
            barrier,
            inc=1,
            device_id={"comp": other, "tile": lax.rem(me + offset + tiles, tiles)},
        )

    high, low = halves(mix_ref[...])
    forward_mix[...] = jnp.concatenate([high, high], axis=1)
    forward_low[...] = low
    high, low = halves(mix_ref[...].T)
    backward_mix[...] = jnp.concatenate([high, high], axis=1)
    backward_low[...] = low

    def edge_copy(side, chunk, slot):
        return pltpu.make_async_remote_copy(
            src_ref=outgoing.at[side, chunk],
            dst_ref=halo.at[slot, side, chunk],
            send_sem=halo_send.at[side, chunk],
            recv_sem=halo_recv.at[slot, side, chunk],
            device_id={"tile": below if side == 0 else above},
        )

    def send_edges(field):
        for chunk in range(chunks):
            cols = pl.ds(chunk * LANES, LANES)
            for side, row in ((0, last), (1, 0)):
                outgoing[side, chunk] = field[0, row, :, cols]
                edge_copy(side, chunk, 0).start()

    def column_mix(x, wide, narrow):
        high, low = halves(x)
        mixed[...] = mm(wide[...], jnp.concatenate([high, low], axis=0)) + mm(narrow[...], high)

    def across(x):
        return pltpu.roll(x, 1, 1) + pltpu.roll(x, lon - 1, 1) - 4.0 * x

    depth = 32

    def forward_row(cur, nxt, row, neighbours):
        column_mix(v[cur, row], forward_mix, forward_low)
        sea = sea_ref[pl.ds(row, 1), :]
        for base in range(0, levels, depth):
            band = pl.ds(base, depth)
            x = v[cur, row, band, :]
            total = across(x)
            for step in neighbours:
                total = total + v[cur, row + step, band, :]
            v[nxt, row, band, :] = sea * (x + mixed[band, :]) + scaled[row, band, :] * total

    def backward_row(cur, nxt, row, neighbours):
        sea = sea_ref[pl.ds(row, 1), :]
        column_mix(sea * w[cur, row], backward_mix, backward_low)
        for base in range(0, levels, depth):
            band = pl.ds(base, depth)
            total = across(g[cur, row, band, :])
            for step in neighbours:
                total = total + g[cur, row + step, band, :]
            value = sea * w[cur, row, band, :] + mixed[band, :] + total
            w[nxt, row, band, :] = value
            if len(neighbours) == 2:
                g[nxt, row, band, :] = scaled[row, band, :] * value

    def section(row_update, edge_update):
        def step(k, carry):
            cur = lax.rem(k, 2)
            nxt = 1 - cur
            row_update(cur, nxt, 0, (1,))
            row_update(cur, nxt, last, (-1,))

            def inner(row, carry):
                row_update(cur, nxt, row, (-1, 1))
                return carry

            lax.fori_loop(1, last, inner, 0)
            for chunk in range(chunks):
                cols = pl.ds(chunk * LANES, LANES)
                for arriving, row in ((0, 0), (1, last)):
                    edge_copy(arriving, chunk, cur).wait_recv()
                    leaving = 1 - arriving
                    edge_copy(leaving, chunk, cur).wait_send()
                    outgoing[leaving, chunk] = edge_update(
                        nxt, row, cols, keep[arriving] * halo[cur, arriving, chunk]
                    )

                    @pl.when(k < STEPS - 1)
                    def _():
                        edge_copy(leaving, chunk, nxt).start()

            return carry

        lax.fori_loop(0, STEPS, step, 0)

    def forward_edge(nxt, row, cols, incoming):
        value = v[nxt, row, :, cols] + scaled[row, :, cols] * incoming
        v[nxt, row, :, cols] = value
        return value

    def backward_edge(nxt, row, cols, incoming):
        value = w[nxt, row, :, cols] + incoming
        w[nxt, row, :, cols] = value
        value = scaled[row, :, cols] * value
        g[nxt, row, :, cols] = value
        return value

    places = [
        (row * chunks + chunk, row, pl.ds(chunk * LANES, LANES))
        for row in range(rows)
        for chunk in range(chunks)
    ]

    loads[0].wait()
    pl.semaphore_wait(barrier, slots + 2)
    send_edges(v)
    loads[1].wait()
    section(forward_row, forward_edge)

    for patch, row, cols in places:
        surface[pl.ds(patch, 1), :] = v[0, row, pl.ds(0, 1), cols]
    out_copies = [
        pltpu.make_async_remote_copy(
            src_ref=surface,
            dst_ref=arrived.at[j],
            send_sem=out_send.at[j],
            recv_sem=out_recv.at[j],
            device_id={"comp": other, "tile": lax.rem(me - offset + tiles, tiles)},
        )
        for j, offset in enumerate(offsets)
    ]
    for copy in out_copies:
        copy.start()
    loads[2].wait()
    loads[3].wait()
    landing = (
        lax.broadcasted_iota(jnp.int32, (blocks, LANES), 1) == landing_col[...]
    ).astype(F32)
    for copy in out_copies:
        copy.wait_recv()
    pick = (
        lax.broadcasted_iota(jnp.int32, (blocks, slots * patches), 1) == source_col[...]
    ).astype(F32).astype(BF16)
    high, low = halves(arrived[...].reshape(slots * patches, LANES))
    picked[...] = mm(pick, high) + mm(pick, low)
    terms[...] = landing

    def remap_block(b, total):
        value = weights[b] * picked[pl.ds(b, 1), :]
        return total + jnp.sum(value, axis=1, keepdims=True) * terms[pl.ds(b, 1), :]

    remapped = lax.fori_loop(
        0, blocks, remap_block, jnp.zeros((LANES, LANES), F32), unroll=8
    ).T
    for patch, row, cols in places:
        v[0, row, pl.ds(0, 1), cols] = (
            v[0, row, pl.ds(0, 1), cols]
            + sea_ref[pl.ds(row, 1), cols] * remapped[patch : patch + 1, :]
        )
    for copy in out_copies:
        copy.wait_send()

    send_edges(v)
    section(forward_row, forward_edge)

    store_final = pltpu.make_async_copy(v.at[0], final_hbm, store_sem.at[0])
    store_final.start()

    def mismatch(row, carry):
        value = v[0, row] - measured[row]
        w[0, row] = value
        g[0, row] = scaled[row] * value
        return carry

    lax.fori_loop(0, rows, mismatch, 0)
    send_edges(g)
    section(backward_row, backward_edge)

    for patch, row, cols in places:
        surface[pl.ds(patch, 1), :] = sea_ref[pl.ds(row, 1), cols] * w[0, row, pl.ds(0, 1), cols]
    high, low = halves(surface[...])
    spot = landing[:, :patches].astype(BF16)
    picked[...] = mm(spot, high) + mm(spot, low)

    def return_block(b, carry):
        high, low = halves(picked[pl.ds(b, 1), :])
        weight_high, weight_low = halves(weights[b])
        terms[pl.ds(b, 1), :] = mm(high, weight_high) + mm(low, weight_high) + mm(high, weight_low)
        return carry

    lax.fori_loop(0, blocks, return_block, 0, unroll=8)
    place = (
        lax.broadcasted_iota(jnp.int32, (slots * patches, blocks), 0) == source_row[...]
    ).astype(F32).astype(BF16)
    high, low = halves(terms[...])
    parcels[...] = (mm(place, high) + mm(place, low)).reshape(slots, patches, LANES)
    back_copies = [
        pltpu.make_async_remote_copy(
            src_ref=parcels.at[j],
            dst_ref=returned.at[j],
            send_sem=back_send.at[j],
            recv_sem=back_recv.at[j],
            device_id={"comp": other, "tile": lax.rem(me + offset + tiles, tiles)},
        )
        for j, offset in enumerate(offsets)
    ]
    for copy in back_copies:
        copy.start()
    for copy in back_copies:
        copy.wait_recv()
    surface[...] = jnp.sum(returned[...], axis=0)
    for patch, row, cols in places:
        value = surface[pl.ds(patch, 1), :]
        w[0, row, pl.ds(0, 1), cols] = w[0, row, pl.ds(0, 1), cols] + value
        g[0, row, pl.ds(0, 1), cols] = (
            g[0, row, pl.ds(0, 1), cols] + scaled[row, pl.ds(0, 1), cols] * value
        )
    for copy in back_copies:
        copy.wait_send()

    send_edges(g)
    section(backward_row, backward_edge)
    store_adjoint = pltpu.make_async_copy(w.at[0], adjoint_hbm, store_sem.at[1])
    store_adjoint.start()
    store_final.wait()
    store_adjoint.wait()


def shards(
    starting_perturbation,
    measured_discrepancy,
    diffusion,
    vert_mix,
    ocean_mask,
    pair_tile,
    pair_patch,
    dest_patch,
    pair_blocks,
    remap_weight,
):
    component = lax.axis_index("comp")
    own_tile = lax.axis_index("tile")
    tiles = lax.axis_size("tile")
    levels, rows, lon = starting_perturbation.shape[1:]
    chunks = lon // LANES
    patches = rows * chunks
    blocks = remap_weight.shape[1]
    pairs = pair_tile.shape[2]
    per_pair = blocks // pairs
    slots = 2 * NEAR

    sea = jnp.where(component == 1, ocean_mask.astype(F32), 1.0)
    by_row = lambda x: jnp.transpose(x[0], (1, 0, 2))
    start = by_row(starting_perturbation)
    scaled = by_row(diffusion * sea[None, None])
    measured = by_row(measured_discrepancy)

    offset = (pair_tile[component, own_tile] - own_tile + tiles) % tiles
    slot = jnp.where(
        offset < NEAR, offset, jnp.where(offset == tiles // 2, FAR, offset - tiles + FAR)
    )
    block_ids = jnp.arange(blocks, dtype=jnp.int32)
    live = block_ids % per_pair < jnp.repeat(pair_blocks[0, 0], per_pair)
    source = jnp.repeat(slot, per_pair) * patches + pair_patch[component, own_tile]
    source = jnp.where(live, source, slots * patches)
    landing = dest_patch[0, 0]

    field = (rows, levels, lon)
    hbm = pl.BlockSpec(memory_space=pl.ANY)
    vmem = pl.BlockSpec(memory_space=pltpu.VMEM)
    dma = pltpu.SemaphoreType.DMA
    final, adjoint = pl.pallas_call(
        lambda *refs: window_kernel(tiles, *refs),
        out_shape=(jax.ShapeDtypeStruct(field, F32), jax.ShapeDtypeStruct(field, F32)),
        in_specs=[hbm] * 4 + [vmem] * 5,
        out_specs=(hbm, hbm),
        scratch_shapes=[
            pltpu.VMEM((2,) + field, F32),
            pltpu.VMEM((2,) + field, F32),
            pltpu.VMEM((2,) + field, F32),
            pltpu.VMEM(field, F32),
            pltpu.VMEM(field, F32),
            pltpu.VMEM((blocks, LANES, LANES), F32),
            pltpu.VMEM((levels, lon), F32),
            pltpu.VMEM((levels, 2 * levels), BF16),
            pltpu.VMEM((levels, levels), BF16),
            pltpu.VMEM((levels, 2 * levels), BF16),
            pltpu.VMEM((levels, levels), BF16),
            pltpu.VMEM((2, chunks, levels, LANES), F32),
            pltpu.VMEM((2, 2, chunks, levels, LANES), F32),
            pltpu.VMEM((patches, LANES), F32),
            pltpu.VMEM((slots, patches, LANES), F32),
            pltpu.VMEM((slots, patches, LANES), F32),
            pltpu.VMEM((slots, patches, LANES), F32),
            pltpu.VMEM((blocks, LANES), F32),
            pltpu.VMEM((blocks, LANES), F32),
            dma((4,)),
            dma((2,)),
            dma((2, chunks)),
            dma((2, 2, chunks)),
            dma((slots,)),
            dma((slots,)),
            dma((slots,)),
            dma((slots,)),
        ],
        compiler_params=pltpu.CompilerParams(
            collective_id=0, has_side_effects=True, vmem_limit_bytes=48 * 1024 * 1024
        ),
        name="window",
    )(
        start,
        measured,
        scaled,
        remap_weight[0],
        sea,
        vert_mix[0],
        source[:, None],
        source[None, :],
        landing[:, None],
    )
    back = lambda x: jnp.transpose(x, (1, 0, 2))[None]
    return (back(final), starting_perturbation + back(adjoint))


def solution(mesh):
    placed = (
        P("comp", None, "tile", None),
        P("comp", None, "tile", None),
        P("comp", None, "tile", None),
        P("comp", None, None),
        P("tile", None),
        P(),
        P(),
        P("comp", "tile", None),
        P("comp", "tile", None),
        P("comp", "tile", None, None),
    )
    return jax.shard_map(
        shards,
        mesh=mesh,
        in_specs=placed,
        out_specs=(P("comp", None, "tile", None), P("comp", None, "tile", None)),
        check_vma=False,
    )
```

profile of v0, /device:TPU:0, one launch (start us, length us, event | category | flops | bytes accessed | tf_op | source)
XLA Modules:
  0.0 163.8 jit_solution(14884960076342743253)
XLA Ops:
  0.6 0.9 add_reduce_fusion
  1.5 0.7 fusion.7
  2.2 0.1 broadcast_in_dim.32
  2.3 0.1 mul.38
  2.4 0.7 broadcast_in_dim.30
  3.1 0.1 reshape.132
  3.2 0.7 compare_select_fusion.3.refs_7_
  3.9 0.7 convert_select_fusion.refs_4_
  4.6 0.1 reshape.133
  4.7 0.1 mul.39
  4.7 0.1 copy.17
  4.9 0.7 copy.18.refs_8_
  5.6 0.0 copy-start.2
  5.6 0.0 copy-start.3
  5.6 4.3 %copy.28 = f32[1,128,8,512]{3,1,2,0:T(8,128)} copy(f32[1,128,8,512]{3,2,1,0:T(8,128)} %param.10) | data formatting | bytes 4194304 | tf_op args[0]
  9.9 0.0 copy-done.2
  9.9 0.0 copy-done.3
  9.9 0.0 copy-start
  9.9 4.5 %fusion = (f32[8,128,512]{2,1,0:T(8,128)}, f32[8,128,512]{2,1,0:T(8,128)}) fusion(f32[1,128,8,512]{3,2,1,0:T(8,128)S(1)} %copy-done.2, f32[8,512]{1,0:T(8,128)S(1)} %convert_select_fusion.refs_4_, f32[1,128,8,512]{3,2,1,0:T(8,128)S(1)} %copy-done.3), kind=kLoop, calls=%fused_computation.2 | loop fusion | flops 524288 | bytes 8404992 | tf_op jit(solution)/shard_map/transpose | solution.py:345
  14.4 0.0 copy-done
  14.4 143.0 %window.1 = (f32[8,128,512]{2,1,0:T(8,128)S(1)}, f32[8,128,512]{2,1,0:T(8,128)S(1)}) custom-call(f32[8,128,512]{2,1,0:T(8,128)} %bitcast.32, f32[8,128,512]{2,1,0:T(8,128)} %get-tuple-element.9.refs_1_, f32[8,128,512]{2,1,0:T(8,128)} %get-tuple-element.8.refs_2_, f32[64,128,128]{2,1,0:T(8,128)} %bitcast.33, f32[8,512]{1,0:T(8,128)S(1)} %convert_select_fusion.refs_4_, ...), custom_call_target="tpu_custom_call" | custom-call | tf_op jit(solution)/shard_map/window/pallas_call | solution.py:364
  157.4 0.0 copy-start.1
  157.4 2.5 %copy.20 = f32[1,128,8,512]{3,2,1,0:T(8,128)} copy(f32[1,128,8,512]{3,1,2,0:T(8,128)S(1)} %bitcast.30) | data formatting | bytes 4194304
  159.9 0.0 copy-done.1
  159.9 1.4 bitcast_add_fusion
  161.3 2.5 %copy.21 = f32[1,128,8,512]{3,2,1,0:T(8,128)} copy(f32[1,128,8,512]{3,1,2,0:T(8,128)S(1)} %bitcast_add_fusion) | data formatting | bytes 4194304
  (2 shorter events, 0.0 us)
Async XLA Ops:
  5.6 4.3 %copy-start.2 = (f32[1,128,8,512]{3,2,1,0:T(8,128)S(1)}, f32[1,128,8,512]{3,2,1,0:T(8,128)}, u32[]{:S(2)}) copy-start(f32[1,128,8,512]{3,2,1,0:T(8,128)} %param.12) | copy-start | bytes 6291460
  5.6 4.3 %copy-start.3 = (f32[1,128,8,512]{3,2,1,0:T(8,128)S(1)}, f32[1,128,8,512]{3,2,1,0:T(8,128)}, u32[]{:S(2)}) copy-start(f32[1,128,8,512]{3,2,1,0:T(8,128)} %param.11) | copy-start | bytes 6291460
  9.9 4.5 %copy-start = (f32[1,128,128]{2,1,0:T(8,128)S(1)}, f32[1,128,128]{2,1,0:T(8,128)}, u32[]{:S(2)}) copy-start(f32[1,128,128]{2,1,0:T(8,128)} %param.13) | copy-start | bytes 196612
  157.4 2.6 %copy-start.1 = (f32[1,128,8,512]{3,2,1,0:T(8,128)S(1)}, f32[1,128,8,512]{3,2,1,0:T(8,128)}, u32[]{:S(2)}) copy-start(f32[1,128,8,512]{3,2,1,0:T(8,128)} %param.10) | copy-start | bytes 6291460
where the time goes:
time: 164 us
  Pallas kernels  143 us (87%)
  local copies, waits for them, and re-layouts  12 us (7%)
  other arithmetic  8.13 us (5%)
    pallas_call x1, Pallas kernels, shards(): pl.pallas_call(lambda *refs: window_kernel(tiles, *refs), out_shape=(jax....  143 us
    unnamed x11, local copies, waits for them, and re-layouts  9.37 us
    transpose x1, other arithmetic, shards(): by_row = lambda x: jnp.transpose(x[0], (1, 0, 2))  4.45 us

commit v1 on v0

v1 whole, which is shorter than its diff:
```python
import jax
import jax.numpy as jnp
from jax import lax
from jax.experimental import pallas as pl
from jax.experimental.pallas import tpu as pltpu
from jax.sharding import PartitionSpec as P

STEPS = 4
LANES = 128
NEAR = 8
FAR = 2 * NEAR - 1
GROUP = 8
PARTS = 2

F32 = jnp.float32
BF16 = jnp.bfloat16


def halves(x):
    high = x.astype(BF16)
    return high, (x - high.astype(F32)).astype(BF16)


def mm(a, b):
    return jnp.dot(a, b, preferred_element_type=F32)


def window_kernel(
    tiles,
    start_hbm,
    measured_hbm,
    diffusion_hbm,
    weight_hbm,
    ocean_hbm,
    mix_hbm,
    pair_tile_hbm,
    pair_patch_hbm,
    dest_patch_hbm,
    pair_blocks_hbm,
    final_hbm,
    gradient_hbm,
    start_raw,
    measured_raw,
    diffusion_raw,
    v,
    w,
    g,
    scaled,
    measured,
    weights,
    sea_ref,
    mixed,
    forward_mix,
    forward_low,
    backward_mix,
    backward_low,
    outgoing,
    halo,
    surface,
    departing,
    arrived,
    parcels,
    returned,
    terms,
    shift_out,
    shift_in,
    picked,
    landing,
    pick,
    place,
    gather,
    collect,
    ocean_ref,
    mix_ref,
    pair_tile,
    pair_patch,
    dest_patch,
    pair_blocks,
    load_sem,
    store_sem,
    halo_send,
    halo_recv,
    out_send,
    out_recv,
    back_send,
    back_recv,
    shift_send,
    shift_recv,
):
    rows, levels, lon = scaled.shape
    chunks = lon // LANES
    blocks = weights.shape[0]
    per_pair = GROUP
    pairs = blocks // per_pair
    slots = 2 * NEAR
    last = rows - 1
    part_levels = levels // PARTS
    me = lax.axis_index("tile")
    component = lax.axis_index("comp")
    other = 1 - component
    above = lax.rem(me + tiles - 1, tiles)
    below = lax.rem(me + 1, tiles)

    offsets = [j if j < NEAR else (tiles // 2 if j == FAR else j - FAR) for j in range(slots)]
    keep = (
        jnp.where(me > 0, 1.0, 0.0).astype(F32),
        jnp.where(me < tiles - 1, 1.0, 0.0).astype(F32),
    )

    loads = [
        pltpu.make_async_copy(start_hbm.at[0], start_raw, load_sem.at[0]),
        pltpu.make_async_copy(diffusion_hbm.at[0], diffusion_raw, load_sem.at[1]),
        pltpu.make_async_copy(measured_hbm.at[0], measured_raw, load_sem.at[2]),
        pltpu.make_async_copy(weight_hbm.at[0], weights, load_sem.at[3]),
        pltpu.make_async_copy(mix_hbm.at[0], mix_ref, load_sem.at[4]),
        pltpu.make_async_copy(ocean_hbm, ocean_ref, load_sem.at[5]),
        pltpu.make_async_copy(pair_tile_hbm, pair_tile, load_sem.at[6]),
        pltpu.make_async_copy(pair_patch_hbm, pair_patch, load_sem.at[7]),
        pltpu.make_async_copy(dest_patch_hbm, dest_patch, load_sem.at[8]),
        pltpu.make_async_copy(pair_blocks_hbm, pair_blocks, load_sem.at[9]),
    ]
    for load in loads:
        load.start()

    barrier = pltpu.get_barrier_semaphore()
    for neighbour in (above, below):
        pl.semaphore_signal(barrier, inc=1, device_id={"tile": neighbour})
    for offset in offsets:
        pl.semaphore_signal(
            barrier,
            inc=1,
            device_id={"comp": other, "tile": lax.rem(me + offset + tiles, tiles)},
        )

    shift_out[...] = jnp.zeros_like(shift_out)
    def edge_copy(side, part, chunk, slot):
        return pltpu.make_async_remote_copy(
            src_ref=outgoing.at[side, part, chunk],
            dst_ref=halo.at[slot, side, part, chunk],
            send_sem=halo_send.at[side, part, chunk],
            recv_sem=halo_recv.at[slot, side, part, chunk],
            device_id={"tile": below if side == 0 else above},
        )

    def send_edges(field, part):
        band = pl.ds(part * part_levels, part_levels)
        for chunk in range(chunks):
            cols = pl.ds(chunk * LANES, LANES)
            for side, row in ((0, last), (1, 0)):
                outgoing[side, part, chunk] = field[0, row, band, cols]
                edge_copy(side, part, chunk, 0).start()

    def shift_copy(phase, side):
        return pltpu.make_async_remote_copy(
            src_ref=shift_out.at[phase, side],
            dst_ref=shift_in.at[phase, side],
            send_sem=shift_send.at[phase, side],
            recv_sem=shift_recv.at[phase, side],
            device_id={"tile": below if side == 0 else above},
        )

    def flip(block):
        return jnp.swapaxes(block, 0, 1)

    def by_level_block(body):
        def step(i, carry):
            body(pl.ds(pl.multiple_of(i * GROUP, GROUP), GROUP))
            return carry

        lax.fori_loop(0, levels // GROUP, step, 0)

    def column_mix(i, x, wide, narrow):
        high, low = halves(x)
        mixed[i] = mm(wide[...], jnp.concatenate([high, low], axis=0)) + mm(narrow[...], high)

    def across(x):
        return pltpu.roll(x, 1, 1) + pltpu.roll(x, lon - 1, 1) - 4.0 * x

    depth = 32

    def forward_rows(cur, nxt, targets):
        for i, (row, _) in enumerate(targets):
            column_mix(i, v[cur, row], forward_mix, forward_low)
        for i, (row, neighbours) in enumerate(targets):
            sea = sea_ref[pl.ds(row, 1), :]
            for base in range(0, levels, depth):
                band = pl.ds(base, depth)
                x = v[cur, row, band, :]
                total = across(x)
                for step in neighbours:
                    total = total + v[cur, row + step, band, :]
                v[nxt, row, band, :] = (
                    sea * (x + mixed[i, band, :]) + scaled[row, band, :] * total
                )

    def backward_rows(cur, nxt, targets):
        for i, (row, _) in enumerate(targets):
            sea = sea_ref[pl.ds(row, 1), :]
            column_mix(i, sea * w[cur, row], backward_mix, backward_low)
        for i, (row, neighbours) in enumerate(targets):
            sea = sea_ref[pl.ds(row, 1), :]
            for base in range(0, levels, depth):
                band = pl.ds(base, depth)
                total = across(g[cur, row, band, :])
                for step in neighbours:
                    total = total + g[cur, row + step, band, :]
                value = sea * w[cur, row, band, :] + mixed[i, band, :] + total
                w[nxt, row, band, :] = value
                if len(neighbours) == 2:
                    g[nxt, row, band, :] = scaled[row, band, :] * value

    def inner_pair(update, cur, nxt, index):
        row = 2 + 2 * index
        update(cur, nxt, ((row, (-1, 1)), (row + 1, (-1, 1))))

    def section(update, edge_update, first, phase, final_edge=None, hook=None, hold=False, go_on=True):
        ending = STEPS - 1

        def pair_loop(lo, hi, src, dst):
            def pair(index, carry):
                inner_pair(update, src, dst, index)
                return carry

            lax.fori_loop(lo, hi, pair, 0)

        if phase is None:
            pair_loop(0, (rows - 4) // 2, 0, 1)

        def step(k, carry):
            cur = lax.rem(k, 2)
            nxt = 1 - cur
            update(
                cur,
                nxt,
                ((0, (1,)), (last, (-1,)), (1, (-1, 1)), (last - 1, (-1, 1))),
            )

            def half(i, carry):
                part = i if first == 0 else PARTS - 1 - i
                band = pl.ds(pl.multiple_of(part * part_levels, part_levels), part_levels)
                turning = jnp.logical_and(k == ending, i == 0)
                if phase is not None:

                    @pl.when(jnp.logical_and(k == 0, part == 0))
                    def _():
                        for side in range(2):
                            shift_copy(phase, side).wait_recv()

                for chunk in range(chunks):
                    cols = pl.ds(chunk * LANES, LANES)
                    for arriving, row in ((0, 0), (1, last)):
                        edge_copy(arriving, part, chunk, cur).wait_recv()
                        leaving = 1 - arriving
                        edge_copy(leaving, part, chunk, cur).wait_send()
                        if phase is not None:

                            @pl.when(jnp.logical_and(k == 0, part == 0))
                            def _():
                                halo[0, arriving, 0, chunk, top, :] = (
                                    halo[0, arriving, 0, chunk, top, :]
                                    + shift_in[phase, arriving, pl.ds(chunk, 1), :]
                                )

                        def emit(edge):
                            outgoing[leaving, part, chunk] = edge(
                                nxt,
                                row,
                                band,
                                cols,
                                keep[arriving] * halo[cur, arriving, part, chunk],
                            )

                        if final_edge is None:
                            emit(edge_update)
                        else:

                            @pl.when(k < ending)
                            def _():
                                emit(edge_update)

                            @pl.when(k == ending)
                            def _():
                                emit(final_edge)

                        if go_on and not hold:
                            edge_copy(leaving, part, chunk, nxt).start()
                        else:

                            @pl.when(jnp.logical_not(turning) if go_on else k < ending)
                            def _():
                                edge_copy(leaving, part, chunk, nxt).start()

                if hook is not None:

                    @pl.when(turning)
                    def _():
                        hook()
                        if hold:
                            for chunk in range(chunks):
                                for side in range(2):
                                    edge_copy(side, part, chunk, nxt).start()

                @pl.when(k < ending)
                def _():
                    if phase is None:
                        inner_pair(update, nxt, cur, i)
                    else:
                        late = jnp.logical_and(k == 0, i == 0)
                        pair_loop(
                            jnp.where(k == 0, 0, i),
                            jnp.where(k == 0, (rows - 4) // 2, i + 1),
                            jnp.where(late, cur, nxt),
                            jnp.where(late, nxt, cur),
                        )

                return carry

            lax.fori_loop(0, PARTS, half, 0)
            return carry

        lax.fori_loop(0, STEPS, step, 0)
        if phase is not None:
            for side in range(2):
                shift_copy(phase, side).wait_send()

    def forward_edge(nxt, row, band, cols, incoming):
        value = v[nxt, row, band, cols] + scaled[row, band, cols] * incoming
        v[nxt, row, band, cols] = value
        return value

    def backward_edge(nxt, row, band, cols, incoming):
        value = w[nxt, row, band, cols] + incoming
        w[nxt, row, band, cols] = value
        value = scaled[row, band, cols] * value
        g[nxt, row, band, cols] = value
        return value

    def turning_edge(nxt, row, band, cols, incoming):
        value = forward_edge(nxt, row, band, cols, incoming) - measured[row, band, cols]
        w[nxt, row, band, cols] = value
        value = scaled[row, band, cols] * value
        g[nxt, row, band, cols] = value
        return value

    places = [
        (row * chunks + chunk, row, chunk, pl.ds(chunk * LANES, LANES))
        for row in range(rows)
        for chunk in range(chunks)
    ]
    top = pl.ds(0, 1)

    loads[0].wait()

    def take_start(band):
        v[0, :, band, :] = flip(start_raw[band])

    by_level_block(take_start)
    pl.semaphore_wait(barrier, slots + 2)
    for part in range(PARTS):
        send_edges(v, part)
    for load in loads[4:]:
        load.wait()
    shift_out[...] = jnp.zeros_like(shift_out)
    sea_ref[...] = jnp.where(component == 1, ocean_ref[...].astype(F32), 1.0)
    high, low = halves(mix_ref[...])
    forward_mix[...] = jnp.concatenate([high, high], axis=1)
    forward_low[...] = low
    high, low = halves(mix_ref[...].T)
    backward_mix[...] = jnp.concatenate([high, high], axis=1)
    backward_low[...] = low
    loads[1].wait()

    def take_diffusion(band):
        block = flip(diffusion_raw[band])
        for row in range(rows):
            scaled[row, band, :] = block[row] * sea_ref[pl.ds(row, 1), :]

    by_level_block(take_diffusion)
    loads[2].wait()

    def take_measured(band):
        measured[:, band, :] = flip(measured_raw[band])

    by_level_block(take_measured)

    def iota(shape, dim):
        return lax.broadcasted_iota(jnp.int32, shape, dim)

    def spread(x, y):
        return lax.dot_general(
            x.astype(F32).astype(BF16),
            y.astype(F32).astype(BF16),
            (((1,), (1,)), ((), ())),
            preferred_element_type=F32,
        )

    exchanged = slots * per_pair
    slot = iota((exchanged, tiles), 0) // per_pair
    shift = jnp.where(
        slot < NEAR, slot, jnp.where(slot == FAR, tiles // 2, slot - FAR)
    )
    asking = lax.rem(me - shift + tiles, tiles)
    asking = jnp.where(iota((exchanged, tiles), 1) == asking, 1, 0)
    hit = spread(asking, jnp.where(pair_tile[other] == me, 1, 0))
    hit = mm(
        hit.astype(BF16),
        jnp.where(iota((pairs, blocks), 1) // per_pair == iota((pairs, blocks), 0), 1.0, 0.0)
        .astype(BF16),
    )
    patch_of = mm(
        asking.astype(F32).astype(BF16), pair_patch[other].astype(F32).astype(BF16)
    )
    same = iota((exchanged, blocks), 0) % per_pair == iota((exchanged, blocks), 1) % per_pair
    patch_of = jnp.sum(
        jnp.where(jnp.logical_and(same, hit > 0.5), patch_of, 0.0), axis=1, keepdims=True
    )
    chosen = jnp.where(
        iota((exchanged, LANES), 1).astype(F32) == patch_of, 1.0, 0.0
    )
    gather[...] = chosen.astype(BF16)
    collect[...] = chosen.T.astype(BF16)

    owner = jnp.where(
        iota((blocks, pairs), 0) // per_pair == iota((blocks, pairs), 1), 1.0, 0.0
    )
    mine = jnp.where(iota((pairs, tiles), 1) == me, pair_tile[component], 0)
    mine = jnp.sum(mine.astype(F32), axis=1, keepdims=True)
    source = mm(
        owner.astype(BF16), jnp.broadcast_to(mine, (pairs, LANES)).astype(BF16)
    ).astype(jnp.int32)
    source = source - me
    source = jnp.where(source < 0, source + tiles, source)
    source = jnp.where(
        source < NEAR, source, jnp.where(source == tiles // 2, FAR, source - tiles + FAR)
    )
    source = source * per_pair + iota((blocks, LANES), 0) % per_pair
    live = jnp.sum(owner * pair_blocks[0].astype(F32), axis=1, keepdims=True)
    live = (iota((blocks, LANES), 0) % per_pair).astype(F32) < live
    chosen = jnp.where(
        jnp.logical_and(live, iota((blocks, LANES), 1) == source), 1.0, 0.0
    )
    pick[...] = chosen.astype(BF16)
    chosen = jnp.concatenate([chosen, jnp.zeros((LANES - blocks, LANES), F32)], axis=0)
    place[...] = chosen.T.astype(BF16)
    spot = jnp.where(
        iota((blocks, blocks), 0) == iota((blocks, blocks), 1), dest_patch[0].astype(F32), 0.0
    )
    spot = jnp.sum(spot, axis=1, keepdims=True)
    landing[...] = jnp.where(iota((blocks, LANES), 1).astype(F32) == spot, 1.0, 0.0)

    def select(chooser, x):
        high, low = halves(x)
        return mm(chooser, high) + mm(chooser, low)

    def slot_rows(j):
        return pl.ds(j * per_pair, per_pair)

    def slot_copies(src, dst, send_sem, recv_sem, sign):
        return [
            pltpu.make_async_remote_copy(
                src_ref=src.at[slot_rows(j)],
                dst_ref=dst.at[slot_rows(j)],
                send_sem=send_sem.at[j],
                recv_sem=recv_sem.at[j],
                device_id={"comp": other, "tile": lax.rem(me + sign * offset + tiles, tiles)},
            )
            for j, offset in enumerate(offsets)
        ]

    def give_surface():
        for patch, row, _, cols in places:
            surface[pl.ds(patch, 1), :] = v[0, row, top, cols]

        departing[...] = select(gather[:, : rows * chunks], surface[...])
        for copy in slot_copies(departing, arrived, out_send, out_recv, -1):
            copy.start()

    section(forward_rows, forward_edge, 0, None, hook=give_surface, hold=True)
    loads[3].wait()
    for copy in slot_copies(departing, arrived, out_send, out_recv, -1):
        copy.wait()
    picked[...] = select(pick[...], arrived[...])

    def remap_block(b, total):
        value = weights[b] * picked[pl.ds(b, 1), :]
        return total + jnp.sum(value, axis=1, keepdims=True) * landing[pl.ds(b, 1), :]

    remapped = lax.fori_loop(
        0, blocks, remap_block, jnp.zeros((LANES, LANES), F32), unroll=8
    ).T

    def shift_edges(phase, value, row, chunk):
        for side, edge in ((0, last), (1, 0)):
            if row == edge:
                shift_out[phase, side, pl.ds(chunk, 1), :] = value

    for patch, row, chunk, cols in places:
        value = sea_ref[pl.ds(row, 1), cols] * remapped[patch : patch + 1, :]
        v[0, row, top, cols] = v[0, row, top, cols] + value
        shift_edges(0, value, row, chunk)
    for side in range(2):
        shift_copy(0, side).start()

    section(forward_rows, forward_edge, 1, 0, final_edge=turning_edge)

    def mismatch(row, carry):
        value = v[0, row] - measured[row]
        w[0, row] = value
        g[0, row] = scaled[row] * value
        return carry

    lax.fori_loop(1, last, mismatch, 0)

    def give_final(band):
        diffusion_raw[band] = flip(v[0, :, band, :])

    by_level_block(give_final)
    stores = [pltpu.make_async_copy(diffusion_raw, final_hbm.at[0], store_sem.at[0])]
    stores[0].start()

    def return_block(b, carry):
        high, low = halves(picked[pl.ds(b, 1), :])
        weight_high, weight_low = halves(weights[b])
        terms[pl.ds(b, 1), :] = (
            mm(high, weight_high) + mm(low, weight_high) + mm(high, weight_low)
        )
        return carry

    def give_terms():
        for patch, row, _, cols in places:
            surface[pl.ds(patch, 1), :] = (
                sea_ref[pl.ds(row, 1), cols] * w[0, row, top, cols]
            )
        picked[...] = select(landing[:, : rows * chunks].astype(BF16), surface[...])
        lax.fori_loop(0, blocks, return_block, 0, unroll=8)
        parcels[...] = select(place[:, :blocks], terms[...])
        for copy in slot_copies(parcels, returned, back_send, back_recv, 1):
            copy.start()

    section(backward_rows, backward_edge, 0, None, hook=give_terms)
    for copy in slot_copies(parcels, returned, back_send, back_recv, 1):
        copy.wait()
    surface[...] = select(collect[: rows * chunks, :], returned[...])
    for patch, row, chunk, cols in places:
        value = surface[pl.ds(patch, 1), :]
        w[0, row, top, cols] = w[0, row, top, cols] + value
        value = scaled[row, top, cols] * value
        g[0, row, top, cols] = g[0, row, top, cols] + value
        shift_edges(1, value, row, chunk)
    for side in range(2):
        shift_copy(1, side).start()

    section(backward_rows, backward_edge, 1, 1, go_on=False)

    cuts = 4
    for cut in range(cuts):
        depth_cut = levels // cuts

        def give_gradient(i, carry):
            band = pl.ds(pl.multiple_of(cut * depth_cut + i * GROUP, GROUP), GROUP)
            measured_raw[band] = start_raw[band] + flip(w[0, :, band, :])
            return carry

        lax.fori_loop(0, depth_cut // GROUP, give_gradient, 0)
        part = pl.ds(cut * depth_cut, depth_cut)
        store = pltpu.make_async_copy(
            measured_raw.at[part], gradient_hbm.at[0, part], store_sem.at[1 + cut]
        )
        store.start()
        stores.append(store)
    for store in stores:
        store.wait()


def shards(
    starting_perturbation,
    measured_discrepancy,
    diffusion,
    vert_mix,
    ocean_mask,
    pair_tile,
    pair_patch,
    dest_patch,
    pair_blocks,
    remap_weight,
):
    tiles = lax.axis_size("tile")
    levels, rows, lon = starting_perturbation.shape[1:]
    chunks = lon // LANES
    patches = rows * chunks
    blocks = remap_weight.shape[1]
    slots = 2 * NEAR
    exchanged = slots * GROUP
    part_levels = levels // PARTS

    raw = (levels, rows, lon)
    field = (rows, levels, lon)
    hbm = pl.BlockSpec(memory_space=pltpu.HBM)
    dma = pltpu.SemaphoreType.DMA
    out = jax.ShapeDtypeStruct((1,) + raw, F32)
    return pl.pallas_call(
        lambda *refs: window_kernel(tiles, *refs),
        out_shape=(out, out),
        in_specs=[hbm] * 10,
        out_specs=(hbm, hbm),
        scratch_shapes=[
            pltpu.VMEM(raw, F32),
            pltpu.VMEM(raw, F32),
            pltpu.VMEM(raw, F32),
            pltpu.VMEM((2,) + field, F32),
            pltpu.VMEM((2,) + field, F32),
            pltpu.VMEM((2,) + field, F32),
            pltpu.VMEM(field, F32),
            pltpu.VMEM(field, F32),
            pltpu.VMEM((blocks, LANES, LANES), F32),
            pltpu.VMEM((rows, lon), F32),
            pltpu.VMEM((4, levels, lon), F32),
            pltpu.VMEM((levels, 2 * levels), BF16),
            pltpu.VMEM((levels, levels), BF16),
            pltpu.VMEM((levels, 2 * levels), BF16),
            pltpu.VMEM((levels, levels), BF16),
            pltpu.VMEM((2, PARTS, chunks, part_levels, LANES), F32),
            pltpu.VMEM((2, 2, PARTS, chunks, part_levels, LANES), F32),
            pltpu.VMEM((patches, LANES), F32),
            pltpu.VMEM((exchanged, LANES), F32),
            pltpu.VMEM((exchanged, LANES), F32),
            pltpu.VMEM((exchanged, LANES), F32),
            pltpu.VMEM((exchanged, LANES), F32),
            pltpu.VMEM((blocks, LANES), F32),
            pltpu.VMEM((2, 2, 8, LANES), F32),
            pltpu.VMEM((2, 2, 8, LANES), F32),
            pltpu.VMEM((blocks, LANES), F32),
            pltpu.VMEM((blocks, LANES), F32),
            pltpu.VMEM((blocks, LANES), BF16),
            pltpu.VMEM((LANES, LANES), BF16),
            pltpu.VMEM((LANES, LANES), BF16),
            pltpu.VMEM((LANES, LANES), BF16),
            pltpu.VMEM((rows, lon), jnp.int32),
            pltpu.VMEM((levels, levels), F32),
            pltpu.VMEM((2, pair_tile.shape[2], tiles), jnp.int32),
            pltpu.VMEM(pair_patch.shape, jnp.int32),
            pltpu.VMEM(dest_patch.shape, jnp.int32),
            pltpu.VMEM(pair_blocks.shape, jnp.int32),
            dma((10,)),
            dma((5,)),
            dma((2, PARTS, chunks)),
            dma((2, 2, PARTS, chunks)),
            dma((slots,)),
            dma((slots,)),
            dma((slots,)),
            dma((slots,)),
            dma((2, 2)),
            dma((2, 2)),
        ],
        compiler_params=pltpu.CompilerParams(
            collective_id=0, has_side_effects=True, vmem_limit_bytes=59 * 1024 * 1024
        ),
        name="window",
    )(
        starting_perturbation,
        measured_discrepancy,
        diffusion,
        remap_weight,
        ocean_mask,
        vert_mix,
        jnp.swapaxes(pair_tile, 1, 2),
        pair_patch,
        dest_patch,
        pair_blocks,
    )


def solution(mesh):
    placed = (
        P("comp", None, "tile", None),
        P("comp", None, "tile", None),
        P("comp", None, "tile", None),
        P("comp", None, None),
        P("tile", None),
        P(),
        P(),
        P("comp", "tile", None),
        P("comp", "tile", None),
        P("comp", "tile", None, None),
    )
    return jax.shard_map(
        shards,
        mesh=mesh,
        in_specs=placed,
        out_specs=(P("comp", None, "tile", None), P("comp", None, "tile", None)),
        check_vma=False,
    )
```

time: 164 us -> 130 us (0.79)
  Pallas kernels: 143 us -> 125 us
  other arithmetic: 8.13 us -> 0 us
  local copies, waits for them, and re-layouts: 12 us -> 4.55 us
    pallas_call x1, Pallas kernels: 143 us -> 125 us  [shards(): pl.pallas_call(lambda *refs: window_kernel(tiles, *refs), out_shape=(out,...]
    unnamed x11 -> x4, local copies, waits for them, and re-layouts: 9.37 us -> 4.55 us
    transpose x1 -> x0, other arithmetic: 4.45 us -> none  [shards(): by_row = lambda x: jnp.transpose(x[0], (1, 0, 2))]
    add x2 -> x0, other arithmetic: 2.23 us -> none  [the longest x1 1.35 us: shards(): return (back(final), starting_perturbation + back(adjoint))]
where the time goes in v1:
time: 130 us
  Pallas kernels  125 us (96%)
  local copies, waits for them, and re-layouts  4.55 us (4%)
    pallas_call x1, Pallas kernels, shards(): pl.pallas_call(lambda *refs: window_kernel(tiles, *refs), out_shape=(out,...  125 us
    unnamed x4, local copies, waits for them, and re-layouts  4.55 us

profile of v1, /device:TPU:0, one launch (start us, length us, event | category | flops | bytes accessed | tf_op | source)
XLA Modules:
  0.0 129.8 jit_solution(5625855736932849259)
XLA Ops:
  0.6 124.6 %window.1 = (f32[1,128,8,512]{3,2,1,0:T(8,128)}, f32[1,128,8,512]{3,2,1,0:T(8,128)}) custom-call(f32[1,128,8,512]{3,2,1,0:T(8,128)} %refs_0_.1, f32[1,128,8,512]{3,2,1,0:T(8,128)} %refs_1_.1, f32[1,128,8,512]{3,2,1,0:T(8,128)} %refs_2_.1, f32[1,64,128,128]{3,2,1,0:T(8,128)} %refs_3_.1, s32[8,512]{1,0:T(8,128)} %refs_4_.1, f32[1,128,128]{2,1,0:T(8,128)} %refs_5_.1, ...), custom_call_target="tpu_custom_call" | custom-call | tf_op jit(solution)/shard_map/window/pallas_call | solution.py:601
  125.3 0.0 copy-start
  125.3 3.2 %copy.14 = f32[1,128,8,512]{3,2,1,0:T(8,128)} copy(f32[1,128,8,512]{3,2,1,0:T(8,128)} %get-tuple-element.4) | data formatting | bytes 4194304
  128.5 0.0 copy-done
  128.5 1.3 %copy.15 = f32[1,128,8,512]{3,2,1,0:T(8,128)} copy(f32[1,128,8,512]{3,2,1,0:T(8,128)S(1)} %copy-done) | data formatting | bytes 4194304
Async XLA Ops:
  125.3 3.2 %copy-start = (f32[1,128,8,512]{3,2,1,0:T(8,128)S(1)}, f32[1,128,8,512]{3,2,1,0:T(8,128)}, u32[]{:S(2)}) copy-start(f32[1,128,8,512]{3,2,1,0:T(8,128)} %get-tuple-element.5) | copy-start | bytes 6291460

commit v2 on v1

--- a/solution.py
+++ b/solution.py
@@ -108,7 +108,11 @@
     )
 
     loads = [
-        pltpu.make_async_copy(start_hbm.at[0], start_raw, load_sem.at[0]),
+        pltpu.make_async_copy(
+            start_hbm.at[0, pl.ds(0, part_levels)],
+            start_raw.at[pl.ds(0, part_levels)],
+            load_sem.at[0],
+        ),
         pltpu.make_async_copy(diffusion_hbm.at[0], diffusion_raw, load_sem.at[1]),
         pltpu.make_async_copy(measured_hbm.at[0], measured_raw, load_sem.at[2]),
         pltpu.make_async_copy(weight_hbm.at[0], weights, load_sem.at[3]),
@@ -119,7 +123,13 @@
         pltpu.make_async_copy(dest_patch_hbm, dest_patch, load_sem.at[8]),
         pltpu.make_async_copy(pair_blocks_hbm, pair_blocks, load_sem.at[9]),
     ]
-    for load in loads:
+    rest = pl.ds(part_levels, levels - part_levels)
+    load_rest = pltpu.make_async_copy(
+        start_hbm.at[0, rest], start_raw.at[rest], load_sem.at[10]
+    )
+    loads[0].start()
+    load_rest.start()
+    for load in loads[1:]:
         load.start()
 
     barrier = pltpu.get_barrier_semaphore()
@@ -162,12 +172,12 @@
     def flip(block):
         return jnp.swapaxes(block, 0, 1)
 
-    def by_level_block(body):
+    def by_level_block(body, lo=0, hi=None):
         def step(i, carry):
             body(pl.ds(pl.multiple_of(i * GROUP, GROUP), GROUP))
             return carry
 
-        lax.fori_loop(0, levels // GROUP, step, 0)
+        lax.fori_loop(lo // GROUP, (levels if hi is None else hi) // GROUP, step, 0)
 
     def column_mix(i, x, wide, narrow):
         high, low = halves(x)
@@ -213,18 +223,8 @@
         row = 2 + 2 * index
         update(cur, nxt, ((row, (-1, 1)), (row + 1, (-1, 1))))
 
-    def section(update, edge_update, first, phase, final_edge=None, hook=None, hold=False, go_on=True):
+    def section(update, edge_update, first, phase, final_edge=None, hook=None, hold=False, go_on=True, idle=()):
         ending = STEPS - 1
-
-        def pair_loop(lo, hi, src, dst):
-            def pair(index, carry):
-                inner_pair(update, src, dst, index)
-                return carry
-
-            lax.fori_loop(lo, hi, pair, 0)
-
-        if phase is None:
-            pair_loop(0, (rows - 4) // 2, 0, 1)
 
         def step(k, carry):
             cur = lax.rem(k, 2)
@@ -232,7 +232,7 @@
             update(
                 cur,
                 nxt,
-                ((0, (1,)), (last, (-1,)), (1, (-1, 1)), (last - 1, (-1, 1))),
+                ((0, (1,)), (last, (-1,))),
             )
 
             def half(i, carry):
@@ -290,6 +290,31 @@
                             def _():
                                 edge_copy(leaving, part, chunk, nxt).start()
 
+                    if chunk == 0:
+
+                        @pl.when(i == 0)
+                        def _():
+                            update(cur, nxt, ((1, (-1, 1)), (last - 1, (-1, 1))))
+
+                        for when, work in enumerate(idle):
+
+                            @pl.when(jnp.logical_and(k == when + 1, i == PARTS - 1))
+                            def _():
+                                work()
+
+                    elif chunk <= (rows - 4) // 2:
+                        early = jnp.logical_or(k == 0, i == 0)
+
+                        @pl.when(jnp.logical_and(k < ending, early))
+                        def _():
+                            late = jnp.logical_and(k == 0, i == 0)
+                            inner_pair(
+                                update,
+                                jnp.where(late, cur, nxt),
+                                jnp.where(late, nxt, cur),
+                                chunk - 1,
+                            )
+
                 if hook is not None:
 
                     @pl.when(turning)
@@ -300,19 +325,6 @@
                                 for side in range(2):
                                     edge_copy(side, part, chunk, nxt).start()
 
-                @pl.when(k < ending)
-                def _():
-                    if phase is None:
-                        inner_pair(update, nxt, cur, i)
-                    else:
-                        late = jnp.logical_and(k == 0, i == 0)
-                        pair_loop(
-                            jnp.where(k == 0, 0, i),
-                            jnp.where(k == 0, (rows - 4) // 2, i + 1),
-                            jnp.where(late, cur, nxt),
-                            jnp.where(late, nxt, cur),
-                        )
-
                 return carry
 
             lax.fori_loop(0, PARTS, half, 0)
@@ -354,9 +366,12 @@
     def take_start(band):
         v[0, :, band, :] = flip(start_raw[band])
 
-    by_level_block(take_start)
+    by_level_block(take_start, 0, part_levels)
     pl.semaphore_wait(barrier, slots + 2)
-    for part in range(PARTS):
+    send_edges(v, 0)
+    load_rest.wait()
+    by_level_block(take_start, part_levels)
+    for part in range(1, PARTS):
         send_edges(v, part)
     for load in loads[4:]:
         load.wait()
@@ -376,12 +391,13 @@
             scaled[row, band, :] = block[row] * sea_ref[pl.ds(row, 1), :]
 
     by_level_block(take_diffusion)
-    loads[2].wait()
 
     def take_measured(band):
         measured[:, band, :] = flip(measured_raw[band])
 
-    by_level_block(take_measured)
+    def measured_rows():
+        loads[2].wait()
+        by_level_block(take_measured)
 
     def iota(shape, dim):
         return lax.broadcasted_iota(jnp.int32, shape, dim)
@@ -394,59 +410,60 @@
             preferred_element_type=F32,
         )
 
-    exchanged = slots * per_pair
-    slot = iota((exchanged, tiles), 0) // per_pair
-    shift = jnp.where(
-        slot < NEAR, slot, jnp.where(slot == FAR, tiles // 2, slot - FAR)
-    )
-    asking = lax.rem(me - shift + tiles, tiles)
-    asking = jnp.where(iota((exchanged, tiles), 1) == asking, 1, 0)
-    hit = spread(asking, jnp.where(pair_tile[other] == me, 1, 0))
-    hit = mm(
-        hit.astype(BF16),
-        jnp.where(iota((pairs, blocks), 1) // per_pair == iota((pairs, blocks), 0), 1.0, 0.0)
-        .astype(BF16),
-    )
-    patch_of = mm(
-        asking.astype(F32).astype(BF16), pair_patch[other].astype(F32).astype(BF16)
-    )
-    same = iota((exchanged, blocks), 0) % per_pair == iota((exchanged, blocks), 1) % per_pair
-    patch_of = jnp.sum(
-        jnp.where(jnp.logical_and(same, hit > 0.5), patch_of, 0.0), axis=1, keepdims=True
-    )
-    chosen = jnp.where(
-        iota((exchanged, LANES), 1).astype(F32) == patch_of, 1.0, 0.0
-    )
-    gather[...] = chosen.astype(BF16)
-    collect[...] = chosen.T.astype(BF16)
-
-    owner = jnp.where(
-        iota((blocks, pairs), 0) // per_pair == iota((blocks, pairs), 1), 1.0, 0.0
-    )
-    mine = jnp.where(iota((pairs, tiles), 1) == me, pair_tile[component], 0)
-    mine = jnp.sum(mine.astype(F32), axis=1, keepdims=True)
-    source = mm(
-        owner.astype(BF16), jnp.broadcast_to(mine, (pairs, LANES)).astype(BF16)
-    ).astype(jnp.int32)
-    source = source - me
-    source = jnp.where(source < 0, source + tiles, source)
-    source = jnp.where(
-        source < NEAR, source, jnp.where(source == tiles // 2, FAR, source - tiles + FAR)
-    )
-    source = source * per_pair + iota((blocks, LANES), 0) % per_pair
-    live = jnp.sum(owner * pair_blocks[0].astype(F32), axis=1, keepdims=True)
-    live = (iota((blocks, LANES), 0) % per_pair).astype(F32) < live
-    chosen = jnp.where(
-        jnp.logical_and(live, iota((blocks, LANES), 1) == source), 1.0, 0.0
-    )
-    pick[...] = chosen.astype(BF16)
-    chosen = jnp.concatenate([chosen, jnp.zeros((LANES - blocks, LANES), F32)], axis=0)
-    place[...] = chosen.T.astype(BF16)
-    spot = jnp.where(
-        iota((blocks, blocks), 0) == iota((blocks, blocks), 1), dest_patch[0].astype(F32), 0.0
-    )
-    spot = jnp.sum(spot, axis=1, keepdims=True)
-    landing[...] = jnp.where(iota((blocks, LANES), 1).astype(F32) == spot, 1.0, 0.0)
+    def selections():
+        exchanged = slots * per_pair
+        slot = iota((exchanged, tiles), 0) // per_pair
+        shift = jnp.where(
+            slot < NEAR, slot, jnp.where(slot == FAR, tiles // 2, slot - FAR)
+        )
+        asking = lax.rem(me - shift + tiles, tiles)
+        asking = jnp.where(iota((exchanged, tiles), 1) == asking, 1, 0)
+        hit = spread(asking, jnp.where(pair_tile[other] == me, 1, 0))
+        hit = mm(
+            hit.astype(BF16),
+            jnp.where(iota((pairs, blocks), 1) // per_pair == iota((pairs, blocks), 0), 1.0, 0.0)
+            .astype(BF16),
+        )
+        patch_of = mm(
+            asking.astype(F32).astype(BF16), pair_patch[other].astype(F32).astype(BF16)
+        )
+        same = iota((exchanged, blocks), 0) % per_pair == iota((exchanged, blocks), 1) % per_pair
+        patch_of = jnp.sum(
+            jnp.where(jnp.logical_and(same, hit > 0.5), patch_of, 0.0), axis=1, keepdims=True
+        )
+        chosen = jnp.where(
+            iota((exchanged, LANES), 1).astype(F32) == patch_of, 1.0, 0.0
+        )
+        gather[...] = chosen.astype(BF16)
+        collect[...] = chosen.T.astype(BF16)
+
+        owner = jnp.where(
+            iota((blocks, pairs), 0) // per_pair == iota((blocks, pairs), 1), 1.0, 0.0
+        )
+        mine = jnp.where(iota((pairs, tiles), 1) == me, pair_tile[component], 0)
+        mine = jnp.sum(mine.astype(F32), axis=1, keepdims=True)
+        source = mm(
+            owner.astype(BF16), jnp.broadcast_to(mine, (pairs, LANES)).astype(BF16)
+        ).astype(jnp.int32)
+        source = source - me
+        source = jnp.where(source < 0, source + tiles, source)
+        source = jnp.where(
+            source < NEAR, source, jnp.where(source == tiles // 2, FAR, source - tiles + FAR)
+        )
+        source = source * per_pair + iota((blocks, LANES), 0) % per_pair
+        live = jnp.sum(owner * pair_blocks[0].astype(F32), axis=1, keepdims=True)
+        live = (iota((blocks, LANES), 0) % per_pair).astype(F32) < live
+        chosen = jnp.where(
+            jnp.logical_and(live, iota((blocks, LANES), 1) == source), 1.0, 0.0
+        )
+        pick[...] = chosen.astype(BF16)
+        chosen = jnp.concatenate([chosen, jnp.zeros((LANES - blocks, LANES), F32)], axis=0)
+        place[...] = chosen.T.astype(BF16)
+        spot = jnp.where(
+            iota((blocks, blocks), 0) == iota((blocks, blocks), 1), dest_patch[0].astype(F32), 0.0
+        )
+        spot = jnp.sum(spot, axis=1, keepdims=True)
+        landing[...] = jnp.where(iota((blocks, LANES), 1).astype(F32) == spot, 1.0, 0.0)
 
     def select(chooser, x):
         high, low = halves(x)
@@ -475,7 +492,15 @@
         for copy in slot_copies(departing, arrived, out_send, out_recv, -1):
             copy.start()
 
-    section(forward_rows, forward_edge, 0, None, hook=give_surface, hold=True)
+    section(
+        forward_rows,
+        forward_edge,
+        0,
+        None,
+        hook=give_surface,
+        hold=True,
+        idle=(measured_rows, selections),
+    )
     loads[3].wait()
     for copy in slot_copies(departing, arrived, out_send, out_recv, -1):
         copy.wait()
@@ -486,7 +511,7 @@
         return total + jnp.sum(value, axis=1, keepdims=True) * landing[pl.ds(b, 1), :]
 
     remapped = lax.fori_loop(
-        0, blocks, remap_block, jnp.zeros((LANES, LANES), F32), unroll=8
+        0, blocks, remap_block, jnp.zeros((LANES, LANES), F32), unroll=16
     ).T
 
     def shift_edges(phase, value, row, chunk):
@@ -514,9 +539,12 @@
     def give_final(band):
         diffusion_raw[band] = flip(v[0, :, band, :])
 
-    by_level_block(give_final)
     stores = [pltpu.make_async_copy(diffusion_raw, final_hbm.at[0], store_sem.at[0])]
-    stores[0].start()
+
+    def final_rows():
+        by_level_block(give_final)
+        stores[0].start()
+
 
     def return_block(b, carry):
         high, low = halves(picked[pl.ds(b, 1), :])
@@ -532,12 +560,14 @@
                 sea_ref[pl.ds(row, 1), cols] * w[0, row, top, cols]
             )
         picked[...] = select(landing[:, : rows * chunks].astype(BF16), surface[...])
-        lax.fori_loop(0, blocks, return_block, 0, unroll=8)
+        lax.fori_loop(0, blocks, return_block, 0, unroll=16)
         parcels[...] = select(place[:, :blocks], terms[...])
         for copy in slot_copies(parcels, returned, back_send, back_recv, 1):
             copy.start()
 
-    section(backward_rows, backward_edge, 0, None, hook=give_terms)
+    section(
+        backward_rows, backward_edge, 0, None, hook=give_terms, idle=(final_rows,)
+    )
     for copy in slot_copies(parcels, returned, back_send, back_recv, 1):
         copy.wait()
     surface[...] = select(collect[: rows * chunks, :], returned[...])
@@ -641,7 +671,7 @@
             pltpu.VMEM(pair_patch.shape, jnp.int32),
             pltpu.VMEM(dest_patch.shape, jnp.int32),
             pltpu.VMEM(pair_blocks.shape, jnp.int32),
-            dma((10,)),
+            dma((11,)),
             dma((5,)),
             dma((2, PARTS, chunks)),
             dma((2, 2, PARTS, chunks)),

time: 130 us -> 127 us (0.977)
  Pallas kernels: 125 us -> 122 us
    pallas_call x1, Pallas kernels: 125 us -> 122 us  [shards(): pl.pallas_call(lambda *refs: window_kernel(tiles, *refs), out_shape=(out,...]
where the time goes in v2:
time: 127 us
  Pallas kernels  122 us (96%)
  local copies, waits for them, and re-layouts  4.55 us (4%)
    pallas_call x1, Pallas kernels, shards(): pl.pallas_call(lambda *refs: window_kernel(tiles, *refs), out_shape=(out,...  122 us
    unnamed x4, local copies, waits for them, and re-layouts  4.55 us

profile of v2, /device:TPU:0, one launch (start us, length us, event | category | flops | bytes accessed | tf_op | source)
XLA Modules:
  0.0 126.8 jit_solution(8003141783177793114)
XLA Ops:
  0.6 121.6 %window.1 = (f32[1,128,8,512]{3,2,1,0:T(8,128)}, f32[1,128,8,512]{3,2,1,0:T(8,128)}) custom-call(f32[1,128,8,512]{3,2,1,0:T(8,128)} %refs_0_.1, f32[1,128,8,512]{3,2,1,0:T(8,128)} %refs_1_.1, f32[1,128,8,512]{3,2,1,0:T(8,128)} %refs_2_.1, f32[1,64,128,128]{3,2,1,0:T(8,128)} %refs_3_.1, s32[8,512]{1,0:T(8,128)} %refs_4_.1, f32[1,128,128]{2,1,0:T(8,128)} %refs_5_.1, ...), custom_call_target="tpu_custom_call" | custom-call | tf_op jit(solution)/shard_map/window/pallas_call | solution.py:631
  122.2 0.0 copy-start
  122.2 3.2 %copy.14 = f32[1,128,8,512]{3,2,1,0:T(8,128)} copy(f32[1,128,8,512]{3,2,1,0:T(8,128)} %get-tuple-element.4) | data formatting | bytes 4194304
  125.5 0.0 copy-done
  125.5 1.3 %copy.15 = f32[1,128,8,512]{3,2,1,0:T(8,128)} copy(f32[1,128,8,512]{3,2,1,0:T(8,128)S(1)} %copy-done) | data formatting | bytes 4194304
Async XLA Ops:
  122.2 3.2 %copy-start = (f32[1,128,8,512]{3,2,1,0:T(8,128)S(1)}, f32[1,128,8,512]{3,2,1,0:T(8,128)}, u32[]{:S(2)}) copy-start(f32[1,128,8,512]{3,2,1,0:T(8,128)} %get-tuple-element.5) | copy-start | bytes 6291460
